TPU v7x, 32 devices: a whole 2x2x4 slice. The times are simulated.
32 devices in a mesh: samp: 16 (over z, y, core), feat: 2 (over x).
Axes of the slice: x: 2, y: 2, z: 4, core: 2. Of those that a mesh axis runs over, the one named last changes fastest.
Arguments:
- grads: bfloat16 [8192, 4096], P('samp', 'feat'), may hold values from -60 to 60
- weights: float32 [8192], P('samp'), may hold values from 0.05 to 6
- targets: float32 [4096, 64], P('feat'), may hold values from -6 to 6
Outputs:
- scores: float32 [8192, 64], P(('samp', 'feat'))
- solution: float32 [4096, 64], P('feat')
- residual: float32 [4096, 64], P('feat')
All inputs are finite; a program needn't handle non-finite values.
Results may differ from a plain program's by a relative error of at most 0.014.
Values may be sent and summed in bfloat16 or wider, within the bound.
A program may use at most 64 MiB of HBM per device.

v0:
```python
import functools
import math

import jax
import jax.numpy as jnp
from jax import lax
from jax.experimental import pallas as pl
from jax.experimental.pallas import tpu as pltpu
from jax.sharding import PartitionSpec as P

ITERS = 2
LANES = 128
VMEM_BYTES = 105 * 2**19
MESH = pl.DeviceIdType.MESH

damping_term = 0.1


def pack_columns(columns):
    dirs = columns[0].shape[0]
    lane = lax.broadcasted_iota(jnp.int32, (dirs, LANES), 1)
    tile = jnp.zeros((dirs, LANES), jnp.float32)
    for position, column in enumerate(columns):
        tile = jnp.where(lane == position, column, tile)
    if dirs < LANES:
        tile = jnp.concatenate([tile, jnp.zeros((LANES - dirs, LANES), jnp.float32)], axis=0)
    return tile.T[:8]


def unpack_columns(tile, count, dirs):
    padded = jnp.concatenate([tile, jnp.zeros((LANES - 8, LANES), jnp.float32)], axis=0).T
    return [padded[:dirs, i : i + 1] for i in range(count)]


def kernel(
    chips, total, full_width,
    grads_hbm, weights_hbm, targets_hbm,
    scores_ref, solution_ref, resid_ref,
    grads_ref, weights_ref, targets_ref,
    rows_out, rows_in, tile_out, tile_in,
    image_f32, image_b16, pair_in, pair_tile_out, pair_tile_in,
    chip_out, chip_in, chip_tiles, gathered,
    load_sem, feat_send, feat_recv, pair_send, pair_recv, chip_send, chip_recv,
):
    samp, feat = lax.axis_index("samp"), lax.axis_index("feat")
    core = lax.rem(samp, 2)
    chip = lax.div(samp, 2)
    dirs, width = targets_ref.shape
    rows_dev = grads_ref.shape[0]
    half = rows_dev // 2
    partner = (samp + 1 - 2 * core, feat)
    mirror = (samp, 1 - feat)
    wide_half = chips * LANES

    def peer(offset):
        other = lax.rem(chip + offset, chips)
        return other, (other * 2 + core, feat)

    loads = [
        pltpu.make_async_copy(targets_hbm, targets_ref, load_sem.at[0]),
        pltpu.make_async_copy(grads_hbm.at[pl.ds(0, half)], grads_ref.at[pl.ds(0, half)], load_sem.at[1]),
        pltpu.make_async_copy(grads_hbm.at[pl.ds(half, half)], grads_ref.at[pl.ds(half, half)], load_sem.at[2]),
        pltpu.make_async_copy(weights_hbm, weights_ref, load_sem.at[3]),
    ]
    for load in loads:
        load.start()

    barrier = pltpu.get_barrier_semaphore()
    for device in [partner, mirror] + [peer(d)[1] for d in range(1, chips)]:
        pl.semaphore_signal(barrier, inc=1, device_id=device, device_id_type=MESH)

    def remote(src, dst, send, recv, device):
        return pltpu.make_async_remote_copy(
            src_ref=src, dst_ref=dst, send_sem=send, recv_sem=recv, device_id=device, device_id_type=MESH
        )

    def lanes_of(which):
        return pl.ds(pl.multiple_of(which * wide_half, wide_half), wide_half)

    own_half, other_half = lanes_of(core), lanes_of(1 - core)
    own_lanes = pl.ds(pl.multiple_of((core * chips + chip) * LANES, LANES), LANES)
    nt = (((1,), (1,)), ((), ()))

    def joined(step, which):
        return jnp.concatenate([gathered[step, which, i] for i in range(chips)], axis=1)

    for step in range(ITERS):
        mine = []
        copies = []
        if step == 0:
            loads[0].wait()
            targets = targets_ref[...]
            packed = targets.astype(jnp.bfloat16)
        else:
            near = joined(step - 1, core)
            started = [
                lax.dot_general(
                    near, grads_ref[h * half : (h + 1) * half, own_half], nt,
                    preferred_element_type=jnp.float32)
                for h in range(2)
            ]
            for i in range(chips):
                remote(
                    gathered.at[step - 1, 1 - core, i], gathered.at[step - 1, 1 - core, i],
                    pair_send.at[step - 1, 2 + i], pair_recv.at[step - 1, 2 + i], partner).wait_recv()
            far = joined(step - 1, 1 - core)
        for h in range(2):
            rows_h = slice(h * half, (h + 1) * half)
            if step == 0:
                loads[1 + h].wait()
                part = lax.dot_general(
                    packed, grads_ref[rows_h, :], nt, preferred_element_type=jnp.float32)
            else:
                part = started[h] + lax.dot_general(
                    far, grads_ref[rows_h, other_half], nt, preferred_element_type=jnp.float32)
            rows_out[step, h] = part.astype(jnp.bfloat16)
            if step == 0 and h == 0:
                pl.semaphore_wait(barrier, chips + 1)
            copies.append(remote(
                rows_out.at[step, h], rows_in.at[step, h],
                feat_send.at[step, h], feat_recv.at[step, h], mirror))
            copies[-1].start()
            mine.append(part)
        if step == 0:
            sums = [jnp.sum(targets * targets, axis=1, keepdims=True)]
        else:
            pieces = [(near, own_half), (far, other_half)]
            sums = [0.0, 0.0]
            for block, lanes in pieces:
                block = block.astype(jnp.float32)
                sums[0] = sums[0] + jnp.sum(block * block, axis=1, keepdims=True)
                sums[1] = sums[1] + jnp.sum(block * targets_ref[:, lanes], axis=1, keepdims=True)
        tile_out[step] = pack_columns(sums)
        copies.append(remote(tile_out.at[step], tile_in.at[step], feat_send.at[step, 2], feat_recv.at[step, 2], mirror))
        copies[-1].start()
        if step == 0:
            loads[3].wait()
            scaled = weights_ref[...] / total
            target_slice = targets_ref[:, own_lanes]

        def finish_sums():
            copies[2].wait()
            return unpack_columns(tile_out[step] + tile_in[step], len(sums), dirs)

        if step == 1:
            sums = finish_sums()
            norm = sums[0]
            ratio = norm / first_norm
            square = norm + 2.0 * ratio * sums[1] + ratio * ratio * first_norm
            direction_slice = resid_slice + ratio * target_slice
        rows, curve = [], 0.0
        toward = mine_image = None
        for h in range(2):
            rows_h = slice(h * half, (h + 1) * half)
            copies[h].wait()
            whole = mine[h] + rows_in[step, h].astype(jnp.float32)
            if step == 1:
                whole = whole + ratio * first_rows[h]
            rows.append(whole)
            weighted = (whole * scaled[:, rows_h]).astype(jnp.bfloat16)
            there = jnp.dot(weighted, grads_ref[rows_h, other_half], preferred_element_type=jnp.float32)
            toward = there if h == 0 else toward + there
            if h == 1:
                for i in range(chips):
                    image_b16[step, i] = toward[:, i * LANES : (i + 1) * LANES].astype(jnp.bfloat16)
                swap = remote(image_b16.at[step], pair_in.at[step], pair_send.at[step, 0], pair_recv.at[step, 0], partner)
                swap.start()
            curve = curve + jnp.sum(weighted.astype(jnp.float32) * whole, axis=1, keepdims=True)
            if h == 1:
                pair_tile_out[step] = pack_columns([curve])
                swap_tile = remote(
                    pair_tile_out.at[step], pair_tile_in.at[step], pair_send.at[step, 1], pair_recv.at[step, 1], partner)
                swap_tile.start()
            here = jnp.dot(weighted, grads_ref[rows_h, own_half], preferred_element_type=jnp.float32)
            mine_image = here if h == 0 else mine_image + here
        if step == 0:
            first_rows = rows
            sums = finish_sums()
            first_norm = norm = square = sums[0]
            resid_slice = direction_slice = target_slice
        swap_tile.wait()
        chip_tiles[step, chip] = pair_tile_out[step] + pair_tile_in[step]
        sends = []
        for d in range(1, chips):
            other, device = peer(d)
            sends.append(remote(
                chip_tiles.at[step, chip], chip_tiles.at[step, chip],
                chip_send.at[step, 1, d], chip_recv.at[step, 1, chip], device))
            sends[-1].start()
        swap.wait()
        for i in range(chips):
            both = mine_image[:, i * LANES : (i + 1) * LANES] + pair_in[step, i].astype(jnp.float32)
            image_f32[i] = both
            chip_out[step, i] = both.astype(jnp.bfloat16)
        for d in range(1, chips):
            other, device = peer(d)
            sends.append(remote(
                chip_out.at[step, other], chip_in.at[step, chip],
                chip_send.at[step, 0, d], chip_recv.at[step, 0, chip], device))
            sends[-1].start()
        for d in range(1, chips):
            other, device = peer(d)
            remote(
                chip_tiles.at[step, other], chip_tiles.at[step, other],
                chip_send.at[step, 1, d], chip_recv.at[step, 1, other], device).wait_recv()
        curve_tile = chip_tiles[step, 0]
        for i in range(1, chips):
            curve_tile = curve_tile + chip_tiles[step, i]
        curvature = unpack_columns(curve_tile, 1, dirs)[0] + damping_term * square
        alpha = norm / curvature
        reduced = image_f32[chip] + damping_term * direction_slice
        for d in range(1, chips):
            other, device = peer(d)
            remote(
                chip_out.at[step, other], chip_in.at[step, other],
                chip_send.at[step, 0, d], chip_recv.at[step, 0, other], device).wait_recv()
            reduced = reduced + chip_in[step, other].astype(jnp.float32)
        resid_slice = resid_slice - alpha * reduced
        gathered[step, core, chip] = resid_slice.astype(jnp.bfloat16)
        spread = []
        for d in range(1, chips):
            other, device = peer(d)
            spread.append(remote(
                gathered.at[step, core, chip], gathered.at[step, core, chip],
                chip_send.at[step, 2, d], chip_recv.at[step, 2, chip], device))
            spread[-1].start()

        def forward(which):
            spread.append(remote(
                gathered.at[step, core, which], gathered.at[step, core, which],
                pair_send.at[step, 2 + which], pair_recv.at[step, 2 + which], partner))
            spread[-1].start()

        forward(chip)
        if step == 0:
            first_alpha = alpha
        else:
            scores = [
                (first_alpha * first_rows[h] + alpha * rows[h]) / math.sqrt(full_width) for h in range(2)
            ]
            scores_ref[...] = jnp.where(feat == 0, scores[0], scores[1])
            for block, lanes in pieces:
                start = targets_ref[:, lanes]
                solution_ref[:, lanes] = first_alpha * start + alpha * (block.astype(jnp.float32) + ratio * start)
        for copy in sends:
            copy.wait_send()
        for d in range(1, chips):
            other, device = peer(d)
            remote(
                gathered.at[step, core, other], gathered.at[step, core, other],
                chip_send.at[step, 2, d], chip_recv.at[step, 2, other], device).wait_recv()
            forward(other)
        if step == ITERS - 1:
            resid_ref[:, own_half] = joined(step, core).astype(jnp.float32)
            for i in range(chips):
                remote(
                    gathered.at[step, 1 - core, i], gathered.at[step, 1 - core, i],
                    pair_send.at[step, 2 + i], pair_recv.at[step, 2 + i], partner).wait_recv()
            resid_ref[:, other_half] = joined(step, 1 - core).astype(jnp.float32)
        for copy in spread:
            copy.wait_send()


def fused(grads, weights, targets):
    rows_dev, feat_cols = grads.shape
    n_samp = lax.axis_size("samp")
    n_feat = lax.axis_size("feat")
    dirs = targets.shape[1]
    chips = n_samp // 2
    f32, b16 = jnp.float32, jnp.bfloat16
    vmem = pl.BlockSpec(memory_space=pltpu.VMEM)
    dma = pltpu.SemaphoreType.DMA
    scores, solved, resid = pl.pallas_call(
        functools.partial(kernel, chips, rows_dev * n_samp, feat_cols * n_feat),
        out_shape=(
            jax.ShapeDtypeStruct((dirs, rows_dev // n_feat), f32),
            jax.ShapeDtypeStruct((dirs, feat_cols), f32),
            jax.ShapeDtypeStruct((dirs, feat_cols), f32),
        ),
        in_specs=[pl.BlockSpec(memory_space=pltpu.HBM)] * 3,
        out_specs=[vmem] * 3,
        scratch_shapes=[
            pltpu.VMEM((rows_dev, feat_cols), b16),
            pltpu.VMEM((1, rows_dev), f32),
            pltpu.VMEM((dirs, feat_cols), f32),
            pltpu.VMEM((ITERS, 2, dirs, rows_dev // 2), b16),
            pltpu.VMEM((ITERS, 2, dirs, rows_dev // 2), b16),
            pltpu.VMEM((ITERS, 8, LANES), f32),
            pltpu.VMEM((ITERS, 8, LANES), f32),
            pltpu.VMEM((chips, dirs, LANES), f32),
            pltpu.VMEM((ITERS, chips, dirs, LANES), b16),
            pltpu.VMEM((ITERS, chips, dirs, LANES), b16),
            pltpu.VMEM((ITERS, 8, LANES), f32),
            pltpu.VMEM((ITERS, 8, LANES), f32),
            pltpu.VMEM((ITERS, chips, dirs, LANES), b16),
            pltpu.VMEM((ITERS, chips, dirs, LANES), b16),
            pltpu.VMEM((ITERS, chips, 8, LANES), f32),
            pltpu.VMEM((ITERS, 2, chips, dirs, LANES), b16),
            dma((4,)),
            dma((ITERS, 3)), dma((ITERS, 3)),
            dma((ITERS, 2 + chips)), dma((ITERS, 2 + chips)),
            dma((ITERS, 3, chips)), dma((ITERS, 3, chips)),
        ],
        compiler_params=pltpu.CompilerParams(collective_id=0, has_side_effects=True, vmem_limit_bytes=VMEM_BYTES),
        name="cg",
    )(grads, weights[None, :], targets.T)
    return scores.T, solved.T, resid.T


def per_device(grads, weights, targets):
    rows_dev, feat_cols = grads.shape
    n_samp = lax.axis_size("samp")
    n_feat = lax.axis_size("feat")
    total = rows_dev * n_samp
    full_width = feat_cols * n_feat
    share = rows_dev // n_feat
    offset = lax.axis_index("feat") * share
    scaled = weights / total
    regrouped = lax.all_to_all(grads, "feat", split_axis=0, concat_axis=1, tiled=True)
    own_weights = lax.dynamic_slice_in_dim(scaled, offset, share, 0)

    def column_norms(resid):
        squares = jnp.sum(resid * resid, axis=0)
        parts = (squares,)
        return lax.psum((parts[0],), "feat")

    solution = jnp.zeros_like(targets)
    resid = targets
    direction = targets
    accum = jnp.zeros((share, targets.shape[1]), jnp.float32)
    norm_now = column_norms(resid)[0]
    for step in range(ITERS):
        packed = direction.astype(jnp.bfloat16)
        sample_rows = jnp.dot(
            regrouped,
            lax.all_gather(packed, "feat", axis=0, tiled=True),
            preferred_element_type=jnp.float32,
        )
        weighted = (sample_rows * own_weights[:, None]).astype(jnp.bfloat16)
        partial_image = lax.psum_scatter(
            lax.dot_general(
                regrouped, weighted, (((0,), (0,)), ((), ())), preferred_element_type=jnp.float32
            ).astype(jnp.bfloat16),
            "feat",
            scatter_dimension=0,
            tiled=True,
        ).astype(jnp.float32)
        own_rows = sample_rows
        apply_own_weights = own_weights
        image = lax.psum(partial_image, "samp") + damping_term * direction
        own_rows, own_weights, image = (own_rows, apply_own_weights, image)
        curvature = lax.psum(jnp.sum(direction * image, axis=0), "feat")
        alpha = norm_now / curvature
        solution = solution + alpha * direction
        resid = resid - alpha * image
        accum = accum + alpha * own_rows
        if step + 1 < ITERS:
            sums = column_norms(resid)
            norm_next = sums[0]
            ratio = norm_next / norm_now
            direction = resid + ratio * direction
            norm_now = norm_next
    scores = accum / math.sqrt(full_width)
    return (scores, solution, resid)


def dispatch(grads, weights, targets):
    rows_dev, feat_cols = grads.shape
    n_samp, n_feat = lax.axis_size("samp"), lax.axis_size("feat")
    fits = (
        n_feat == 2
        and n_samp % 2 == 0
        and n_samp >= 4
        and feat_cols == n_samp * LANES
        and rows_dev % (2 * LANES) == 0
        and targets.shape[1] % 16 == 0
        and targets.shape[1] <= LANES
    )
    return (fused if fits else per_device)(grads, weights, targets)


def solution(mesh):
    return jax.shard_map(
        dispatch,
        mesh=mesh,
        in_specs=(P("samp", "feat"), P("samp"), P("feat", None)),
        out_specs=(P(("samp", "feat"), None), P("feat", None), P("feat", None)),
        check_vma=False,
    )
```

profile of v0, /device:TPU:0, one launch (start us, length us, event | category | flops | bytes accessed | tf_op | source)
XLA Modules:
  0.0 44.8 jit_solution(7311338441026654630)
XLA Ops:
  0.6 0.0 copy-start
  0.6 0.7 %copy-done = f32[512]{0:T(512)S(1)} copy-done((f32[512]{0:T(512)S(1)}, f32[512]{0:T(512)}, u32[]{:S(2)}) %copy-start) | copy-done | bytes 2072
  1.3 41.3 %cg.1 = (f32[64,256]{1,0:T(8,128)S(1)}, f32[64,2048]{1,0:T(8,128)S(1)}, f32[64,2048]{1,0:T(8,128)S(1)}) custom-call(bf16[512,2048]{1,0:T(8,128)(2,1)} %grads_hbm.1, f32[1,512]{1,0:T(1,128)S(1)} %bitcast.8, f32[64,2048]{1,0:T(8,128)} %bitcast.9), custom_call_target="tpu_custom_call" | custom-call | tf_op jit(solution)/shard_map/cg/pallas_call | solution.py:273
  42.6 0.6 %copy.9 = f32[256,64]{0,1:T(8,128)} copy(f32[256,64]{0,1:T(8,128)S(1)} %bitcast.7) | data formatting | bytes 131072
  43.2 0.8 %copy.10 = f32[2048,64]{0,1:T(8,128)} copy(f32[2048,64]{0,1:T(8,128)S(1)} %bitcast.6) | data formatting | bytes 1048576
  44.0 0.8 %copy.11 = f32[2048,64]{0,1:T(8,128)} copy(f32[2048,64]{0,1:T(8,128)S(1)} %bitcast.5) | data formatting | bytes 1048576
Async XLA Ops:
  0.6 0.7 %copy-start = (f32[512]{0:T(512)S(1)}, f32[512]{0:T(512)}, u32[]{:S(2)}) copy-start(f32[512]{0:T(512)} %param.4) | copy-start | bytes 6148
where the time goes:
time: 45 us; the launch traced here: 44.8 us
  Pallas kernels  41.3 us (92%)
  local copies, waits for them, and re-layouts  2.89 us (6%)
  between operations  0.65 us (1%)
    pallas_call x1, Pallas kernels, fused(): pl.pallas_call(functools.partial(kernel, chips, rows_dev * n_samp, feat_c...  41.3 us
    unnamed x5, local copies, waits for them, and re-layouts  2.89 us

commit v1 on v0

--- a/solution.py
+++ b/solution.py
@@ -11,6 +11,7 @@
 ITERS = 2
 LANES = 128
 VMEM_BYTES = 105 * 2**19
+STORE_BYTES = 2**22
 MESH = pl.DeviceIdType.MESH
 
 damping_term = 0.1
@@ -261,6 +262,28 @@
             copy.wait_send()
 
 
+def store_kernel(*refs):
+    count = len(refs) // 2
+    sem = refs[-1]
+    copies = [pltpu.make_async_copy(refs[i], refs[count + i], sem.at[i]) for i in range(count)]
+    for copy in copies:
+        copy.start()
+    for copy in copies:
+        copy.wait()
+
+
+def write_out(*arrays):
+    return pl.pallas_call(
+        store_kernel,
+        out_shape=tuple(jax.ShapeDtypeStruct(a.shape, a.dtype) for a in arrays),
+        in_specs=[pl.BlockSpec(memory_space=pltpu.VMEM)] * len(arrays),
+        out_specs=[pl.BlockSpec(memory_space=pltpu.HBM)] * len(arrays),
+        scratch_shapes=[pltpu.SemaphoreType.DMA((len(arrays),))],
+        compiler_params=pltpu.CompilerParams(vmem_limit_bytes=STORE_BYTES),
+        name="store",
+    )(*arrays)
+
+
 def fused(grads, weights, targets):
     rows_dev, feat_cols = grads.shape
     n_samp = lax.axis_size("samp")
@@ -304,6 +327,7 @@
         compiler_params=pltpu.CompilerParams(collective_id=0, has_side_effects=True, vmem_limit_bytes=VMEM_BYTES),
         name="cg",
     )(grads, weights[None, :], targets.T)
+    scores, solved, resid = write_out(scores, solved, resid)
     return scores.T, solved.T, resid.T
 
 

time: 45 us -> 43.8 us (0.973)
  local copies, waits for them, and re-layouts: 2.89 us -> 0.67 us
  Pallas kernels: 41.3 us -> 42.3 us
    unnamed x5 -> x2, local copies, waits for them, and re-layouts: 2.89 us -> 0.67 us
    pallas_call x0 -> x1, Pallas kernels: none -> 1.02 us  [write_out(): pl.pallas_call(store_kernel, out_shape=tuple((jax.ShapeDtypeStruct(a.shap...]
where the time goes in v1:
time: 43.8 us; the launch traced here: 43.6 us
  Pallas kernels  42.3 us (97%)
  local copies, waits for them, and re-layouts  0.67 us (2%)
  between operations  0.65 us (1%)
    pallas_call x1, Pallas kernels, fused(): pl.pallas_call(functools.partial(kernel, chips, rows_dev * n_samp, feat_c...  41.3 us
    pallas_call x1, Pallas kernels, write_out(): pl.pallas_call(store_kernel, out_shape=tuple((jax.ShapeDtypeStruct(a.shap...  1.02 us

profile of v1, /device:TPU:0, one launch (start us, length us, event | category | flops | bytes accessed | tf_op | source)
XLA Modules:
  0.0 43.6 jit_solution(1112835613274788994)
XLA Ops:
  0.6 0.0 copy-start
  0.6 0.7 %copy-done = f32[512]{0:T(512)S(1)} copy-done((f32[512]{0:T(512)S(1)}, f32[512]{0:T(512)}, u32[]{:S(2)}) %copy-start) | copy-done | bytes 2072
  1.3 41.3 %cg.1 = (f32[64,256]{1,0:T(8,128)S(1)}, f32[64,2048]{1,0:T(8,128)S(1)}, f32[64,2048]{1,0:T(8,128)S(1)}) custom-call(bf16[512,2048]{1,0:T(8,128)(2,1)} %grads_hbm.1, f32[1,512]{1,0:T(1,128)S(1)} %bitcast.5, f32[64,2048]{1,0:T(8,128)} %bitcast.6), custom_call_target="tpu_custom_call" | custom-call | tf_op jit(solution)/shard_map/cg/pallas_call | solution.py:296
  42.6 1.0 %store.1 = (f32[64,256]{1,0:T(8,128)}, f32[64,2048]{1,0:T(8,128)}, f32[64,2048]{1,0:T(8,128)}) custom-call(f32[64,256]{1,0:T(8,128)S(1)} %get-tuple-element.9.refs_0_, f32[64,2048]{1,0:T(8,128)S(1)} %get-tuple-element.10.refs_1_, f32[64,2048]{1,0:T(8,128)S(1)} %get-tuple-element.11.refs_2_), custom_call_target="tpu_custom_call" | custom-call | tf_op jit(solution)/shard_map/store/pallas_call | solution.py:276
Async XLA Ops:
  0.6 0.7 %copy-start = (f32[512]{0:T(512)S(1)}, f32[512]{0:T(512)}, u32[]{:S(2)}) copy-start(f32[512]{0:T(512)} %param.4) | copy-start | bytes 6148

commit v2 on v1

v2 whole, which is shorter than its diff:
```python
import functools
import math

import jax
import jax.numpy as jnp
from jax import lax
from jax.experimental import pallas as pl
from jax.experimental.pallas import tpu as pltpu
from jax.sharding import PartitionSpec as P

ITERS = 2
CHUNK = 16
LANES = 128
VMEM_BYTES = 105 * 2**19
STORE_BYTES = 2**22
MESH = pl.DeviceIdType.MESH

damping_term = 0.1


def kernel(
    total, full_width,
    grads_hbm, weights_hbm, targets_hbm,
    scores_ref, solution_ref, resid_ref,
    grads_ref, weights_ref, targets_ref,
    rows_out, rows_in, first_rows, second_rows,
    norms_out, norms_in, sums_out, sums_in,
    part_out, part_in, gathered, curve_out, curve_in,
    load_sem, x_send, x_recv, part_send, part_recv, gather_send, gather_recv, curve_send, curve_recv,
):
    samp, feat = lax.axis_index("samp"), lax.axis_index("feat")
    n_samp = part_in.shape[1]
    chips = n_samp // 2
    core, chip = lax.rem(samp, 2), lax.div(samp, 2)
    dirs = targets_ref.shape[0]
    rows_dev = grads_ref.shape[0]
    half = rows_dev // 2
    pair = 2 * LANES
    groups = [slice(i, min(i + CHUNK, dirs)) for i in range(0, dirs, CHUNK)]
    count = len(groups)
    f32, b16 = jnp.float32, jnp.bfloat16
    nt = (((1,), (1,)), ((), ()))
    mirror = (samp, 1 - feat)

    def flipped(index, mask, bits):
        for b in range(bits):
            if (mask >> b) & 1:
                index = index + (1 - 2 * lax.rem(lax.div(index, 2**b), 2)) * 2**b
        return index

    bits = (chips - 1).bit_length()
    peer_chip = [flipped(chip, j, bits) for j in range(chips)]
    near_first = sorted(range(chips), key=lambda j: j // 2 + j % 2)
    far_first = near_first[::-1]

    def peer(j, c):
        to = core if c == 0 else 1 - core
        return to, (peer_chip[j] * 2 + to, feat)

    others = [(j, c) for j in far_first for c in (0, 1) if (j, c) != (0, 0)]

    loads = [
        pltpu.make_async_copy(targets_hbm, targets_ref, load_sem.at[0]),
        pltpu.make_async_copy(grads_hbm.at[pl.ds(0, half)], grads_ref.at[pl.ds(0, half)], load_sem.at[1]),
        pltpu.make_async_copy(grads_hbm.at[pl.ds(half, half)], grads_ref.at[pl.ds(half, half)], load_sem.at[2]),
        pltpu.make_async_copy(weights_hbm, weights_ref, load_sem.at[3]),
    ]
    for load in loads:
        load.start()

    barrier = pltpu.get_barrier_semaphore()
    for device in [mirror] + [peer(j, c)[1] for j, c in others]:
        pl.semaphore_signal(barrier, inc=1, device_id=device, device_id_type=MESH)

    def remote(src, dst, send, recv, device):
        return pltpu.make_async_remote_copy(
            src_ref=src, dst_ref=dst, send_sem=send, recv_sem=recv, device_id=device, device_id_type=MESH
        )

    def rows_of(g):
        return pl.ds(groups[g].start, groups[g].stop - groups[g].start)

    def pair_lanes(j):
        return pl.ds(pl.multiple_of(peer_chip[j] * pair, pair), pair)

    own_lanes = pl.ds(pl.multiple_of(samp * LANES, LANES), LANES)

    def x_copy(s, g, kind):
        if kind == 0:
            src, dst = rows_out.at[s, rows_of(g)], rows_in.at[s, rows_of(g)]
        elif s == 0:
            src, dst = norms_out.at[rows_of(g)], norms_in.at[rows_of(g)]
        else:
            src, dst = sums_out.at[rows_of(g)], sums_in.at[rows_of(g)]
        return remote(src, dst, x_send.at[s, g, kind], x_recv.at[s, g, kind], mirror)

    def part_copy(s, g, j, c):
        to, device = peer(j, c)
        return remote(
            part_out.at[s, j, to, rows_of(g)], part_in.at[s, 2 * j + c, rows_of(g)],
            part_send.at[s, g], part_recv.at[s, g], device)

    def part_all(s, g):
        ref = part_in.at[s, pl.ds(1, n_samp - 1), rows_of(g)]
        return remote(ref, ref, part_send.at[s, g], part_recv.at[s, g], mirror)

    def tile_copy(s, g, j, c):
        to, device = peer(j, c)
        ref = gathered.at[s, chip, core, rows_of(g)]
        return remote(ref, ref, gather_send.at[s, g], gather_recv.at[s, g, j], device)

    def tile_wait(s, g, j):
        if j == 0:
            ref = gathered.at[s, chip, 1 - core, rows_of(g)]
        else:
            ref = gathered.at[s, peer_chip[j], pl.ds(0, 2), rows_of(g)]
        remote(ref, ref, gather_send.at[s, g], gather_recv.at[s, g, j], mirror).wait_recv()

    def curve_copy(g, j, c):
        to, device = peer(j, c)
        return remote(
            curve_out.at[g, pl.ds(0, 1)], curve_in.at[g, pl.ds(2 * j + c, 1)],
            curve_send.at[g], curve_recv.at[g], device)

    def curve_all(g):
        ref = curve_in.at[g, pl.ds(1, n_samp - 1)]
        return remote(ref, ref, curve_send.at[g], curve_recv.at[g], mirror)

    def lane_sum(block):
        folded = block[:, :LANES]
        for i in range(1, block.shape[1] // LANES):
            folded = folded + block[:, i * LANES : (i + 1) * LANES]
        return folded

    def column(block):
        return jnp.sum(block, axis=1, keepdims=True)

    def diagonal(size):
        shape = (size, LANES)
        return lax.broadcasted_iota(jnp.int32, shape, 0) == lax.broadcasted_iota(jnp.int32, shape, 1)

    loads[0].wait()
    targets = targets_ref[...]
    packed = targets.astype(b16)
    for h in range(2):
        part_h = slice(h * half, (h + 1) * half)
        loads[1 + h].wait()
        part = lax.dot_general(packed, grads_ref[part_h, :], nt, preferred_element_type=f32)
        first_rows[:, part_h] = part
        rows_out[0, :, part_h] = part.astype(b16)
    pl.semaphore_wait(barrier, n_samp)
    for g in range(count):
        x_copy(0, g, 0).start()
    norms_out[...] = lane_sum(targets * targets)
    for g in range(count):
        x_copy(0, g, 1).start()
    loads[3].wait()
    scaled = weights_ref[...] / total
    state = [dict() for _ in range(count)]

    def exchange(s, g):
        now, rows = state[g], groups[g]
        if s == 0:
            x_copy(0, g, 0).wait_recv()
            whole = first_rows[rows, :] + rows_in[0, rows, :].astype(f32)
            first_rows[rows, :] = whole
        else:
            x_copy(0, g, 1).wait_recv()
            x_copy(1, g, 1).wait_recv()
            norm0 = column(norms_out[rows, :] + norms_in[rows, :])
            both = sums_out[rows, :] + sums_in[rows, :]
            along, square = column(both[:, :LANES]), column(both[:, LANES:])
            alpha0 = norm0 / along
            cross = norm0 - alpha0 * along
            norm1 = cross - alpha0 * (along - alpha0 * square)
            ratio = norm1 / norm0
            now.update(alpha0=alpha0, norm1=norm1, ratio=ratio,
                       length=norm1 + 2.0 * ratio * cross + ratio * ratio * norm0)
            x_copy(1, g, 0).wait_recv()
            image_rows = second_rows[rows, :] + rows_in[1, rows, :].astype(f32)
            whole = (1.0 + ratio) * first_rows[rows, :] - alpha0 * image_rows
            second_rows[rows, :] = whole
        weighted = (whole * scaled).astype(b16)
        for j in far_first:
            image = jnp.dot(weighted, grads_ref[:, pair_lanes(j)], preferred_element_type=f32)
            if j == 0:
                now["own"] = jnp.where(core == 0, image[:, :LANES], image[:, LANES:])
            for c in range(2):
                part_out[s, j, c, rows, :] = image[:, c * LANES : (c + 1) * LANES].astype(b16)
            for c in range(2):
                if (j, c) != (0, 0):
                    part_copy(s, g, j, c).start()
        if s == 1:
            size = rows.stop - rows.start
            curve = column(lane_sum(weighted.astype(f32) * whole))
            line = jnp.sum(jnp.where(diagonal(size), curve, 0.0), axis=0, keepdims=True)
            curve_out[g, 0:1, :] = line
            curve_in[g, 0:1, :] = line
            for j, c in others:
                curve_copy(g, j, c).start()

    def reduce(s, g):
        now, rows = state[g], groups[g]
        target = targets_ref[rows, own_lanes]
        if s == 1:
            curve_all(g).wait_recv()
            size = rows.stop - rows.start
            line = jnp.sum(curve_in[g], axis=0, keepdims=True)
            curve = column(jnp.where(diagonal(size), line, 0.0))
            now["alpha1"] = now["norm1"] / (curve + damping_term * now["length"])
            resid = target - now["alpha0"] * now["image0"]
            direction = resid + now["ratio"] * target
        else:
            direction = target
        part_all(s, g).wait_recv()
        image = now["own"] + damping_term * direction
        for k in range(1, n_samp):
            image = image + part_in[s, k, rows, :].astype(f32)
        if s == 0:
            now["image0"] = image
            tile = image
        else:
            tile = resid - now["alpha1"] * image
        gathered[s, chip, core, rows, :] = tile.astype(b16)
        for j, c in others:
            tile_copy(s, g, j, c).start()

    def gather(s, g):
        now, rows = state[g], groups[g]
        if s == 0:
            mine = along = square = 0.0
            for j in near_first:
                tile_wait(0, g, j)
                block = jnp.concatenate([gathered[0, peer_chip[j], c, rows, :] for c in range(2)], axis=1)
                mine = mine + lax.dot_general(
                    block, grads_ref[:, pair_lanes(j)], nt, preferred_element_type=f32)
                block = block.astype(f32)
                along = along + lane_sum(block * targets_ref[rows, pair_lanes(j)])
                square = square + lane_sum(block * block)
            sums_out[rows, :] = jnp.concatenate([along, square], axis=1)
            x_copy(1, g, 1).start()
            rows_out[1, rows, :] = mine.astype(b16)
            x_copy(1, g, 0).start()
            second_rows[rows, :] = mine
        else:
            for j in near_first:
                tile_wait(1, g, j)
                for c in range(2):
                    lanes = pl.ds(pl.multiple_of(peer_chip[j] * pair + c * LANES, LANES), LANES)
                    resid_ref[rows, lanes] = gathered[1, peer_chip[j], c, rows, :].astype(f32)

    def finish(g):
        now, rows = state[g], groups[g]
        alpha0, alpha1 = now["alpha0"], now["alpha1"]
        share = rows_dev // 2
        scores = (alpha0 * first_rows[rows, :] + alpha1 * second_rows[rows, :]) / math.sqrt(full_width)
        scores_ref[rows, :] = jnp.where(feat == 0, scores[:, :share], scores[:, share:])
        start_part = alpha0 + alpha1 * (1.0 + now["ratio"])
        image_part = alpha1 * alpha0
        for i in range(chips):
            for c in range(2):
                lanes = slice(i * pair + c * LANES, i * pair + (c + 1) * LANES)
                solution_ref[rows, lanes] = (
                    start_part * targets_ref[rows, lanes] - image_part * gathered[0, i, c, rows, :].astype(f32))

    for step in order(count):
        stage, *where = step
        {"exchange": exchange, "reduce": reduce, "gather": gather, "finish": finish}[stage](*where)
    for g in range(count):
        for s in range(ITERS):
            for kind in range(2):
                x_copy(s, g, kind).wait_send()
            part_all(s, g).wait_send()
            part_ref = part_in.at[s, pl.ds(1, n_samp - 1), rows_of(g)]
            remote(part_ref, part_ref, gather_send.at[s, g], gather_send.at[s, g], mirror).wait_send()
        curve_all(g).wait_send()


def order(count):
    steps = []
    all_of = range(count)
    steps += [("exchange", 0, g) for g in all_of]
    steps += [("reduce", 0, g) for g in all_of]
    lag = max(1, count - 1)
    gathers, exchanges = list(all_of), list(all_of)
    steps += [("gather", 0, g) for g in gathers[:lag]]
    for g in exchanges:
        steps.append(("exchange", 1, g))
        if lag + g < count:
            steps.append(("gather", 0, lag + g))
    steps += [("reduce", 1, g) for g in all_of]
    steps += [("finish", g) for g in all_of]
    steps += [("gather", 1, g) for g in all_of]
    return steps


def store_kernel(*refs):
    count = len(refs) // 2
    sem = refs[-1]
    copies = [pltpu.make_async_copy(refs[i], refs[count + i], sem.at[i]) for i in range(count)]
    for copy in copies:
        copy.start()
    for copy in copies:
        copy.wait()


def write_out(*arrays):
    return pl.pallas_call(
        store_kernel,
        out_shape=tuple(jax.ShapeDtypeStruct(a.shape, a.dtype) for a in arrays),
        in_specs=[pl.BlockSpec(memory_space=pltpu.VMEM)] * len(arrays),
        out_specs=[pl.BlockSpec(memory_space=pltpu.HBM)] * len(arrays),
        scratch_shapes=[pltpu.SemaphoreType.DMA((len(arrays),))],
        compiler_params=pltpu.CompilerParams(vmem_limit_bytes=STORE_BYTES),
        name="store",
    )(*arrays)


def fused(grads, weights, targets):
    rows_dev, feat_cols = grads.shape
    n_samp = lax.axis_size("samp")
    n_feat = lax.axis_size("feat")
    dirs = targets.shape[1]
    chips = n_samp // 2
    count = -(-dirs // CHUNK)
    f32, b16 = jnp.float32, jnp.bfloat16
    vmem = pl.BlockSpec(memory_space=pltpu.VMEM)
    dma = pltpu.SemaphoreType.DMA
    scores, solved, resid = pl.pallas_call(
        functools.partial(kernel, rows_dev * n_samp, feat_cols * n_feat),
        out_shape=(
            jax.ShapeDtypeStruct((dirs, rows_dev // n_feat), f32),
            jax.ShapeDtypeStruct((dirs, feat_cols), f32),
            jax.ShapeDtypeStruct((dirs, feat_cols), f32),
        ),
        in_specs=[pl.BlockSpec(memory_space=pltpu.HBM)] * 3,
        out_specs=[vmem] * 3,
        scratch_shapes=[
            pltpu.VMEM((rows_dev, feat_cols), b16),
            pltpu.VMEM((1, rows_dev), f32),
            pltpu.VMEM((dirs, feat_cols), f32),
            pltpu.VMEM((ITERS, dirs, rows_dev), b16),
            pltpu.VMEM((ITERS, dirs, rows_dev), b16),
            pltpu.VMEM((dirs, rows_dev), f32),
            pltpu.VMEM((dirs, rows_dev), f32),
            pltpu.VMEM((dirs, LANES), f32),
            pltpu.VMEM((dirs, LANES), f32),
            pltpu.VMEM((dirs, 2 * LANES), f32),
            pltpu.VMEM((dirs, 2 * LANES), f32),
            pltpu.VMEM((ITERS, chips, 2, dirs, LANES), b16),
            pltpu.VMEM((ITERS, n_samp, dirs, LANES), b16),
            pltpu.VMEM((ITERS, chips, 2, dirs, LANES), b16),
            pltpu.VMEM((count, 8, LANES), f32),
            pltpu.VMEM((count, n_samp, LANES), f32),
            dma((4,)),
            dma((ITERS, count, 2)), dma((ITERS, count, 2)),
            dma((ITERS, count)), dma((ITERS, count)),
            dma((ITERS, count)), dma((ITERS, count, chips)),
            dma((count,)), dma((count,)),
        ],
        compiler_params=pltpu.CompilerParams(collective_id=0, has_side_effects=True, vmem_limit_bytes=VMEM_BYTES),
        name="cg",
    )(grads, pltpu.with_memory_space_constraint(weights[None, :], pltpu.HBM), targets.T)
    scores, solved, resid = write_out(scores, solved, resid)
    return scores.T, solved.T, resid.T


def per_device(grads, weights, targets):
    rows_dev, feat_cols = grads.shape
    n_samp = lax.axis_size("samp")
    n_feat = lax.axis_size("feat")
    total = rows_dev * n_samp
    full_width = feat_cols * n_feat
    share = rows_dev // n_feat
    offset = lax.axis_index("feat") * share
    scaled = weights / total
    regrouped = lax.all_to_all(grads, "feat", split_axis=0, concat_axis=1, tiled=True)
    own_weights = lax.dynamic_slice_in_dim(scaled, offset, share, 0)

    def column_norms(resid):
        squares = jnp.sum(resid * resid, axis=0)
        parts = (squares,)
        return lax.psum((parts[0],), "feat")

    solution = jnp.zeros_like(targets)
    resid = targets
    direction = targets
    accum = jnp.zeros((share, targets.shape[1]), jnp.float32)
    norm_now = column_norms(resid)[0]
    for step in range(ITERS):
        packed = direction.astype(jnp.bfloat16)
        sample_rows = jnp.dot(
            regrouped,
            lax.all_gather(packed, "feat", axis=0, tiled=True),
            preferred_element_type=jnp.float32,
        )
        weighted = (sample_rows * own_weights[:, None]).astype(jnp.bfloat16)
        partial_image = lax.psum_scatter(
            lax.dot_general(
                regrouped, weighted, (((0,), (0,)), ((), ())), preferred_element_type=jnp.float32
            ).astype(jnp.bfloat16),
            "feat",
            scatter_dimension=0,
            tiled=True,
        ).astype(jnp.float32)
        own_rows = sample_rows
        apply_own_weights = own_weights
        image = lax.psum(partial_image, "samp") + damping_term * direction
        own_rows, own_weights, image = (own_rows, apply_own_weights, image)
        curvature = lax.psum(jnp.sum(direction * image, axis=0), "feat")
        alpha = norm_now / curvature
        solution = solution + alpha * direction
        resid = resid - alpha * image
        accum = accum + alpha * own_rows
        if step + 1 < ITERS:
            sums = column_norms(resid)
            norm_next = sums[0]
            ratio = norm_next / norm_now
            direction = resid + ratio * direction
            norm_now = norm_next
    scores = accum / math.sqrt(full_width)
    return (scores, solution, resid)


def dispatch(grads, weights, targets):
    rows_dev, feat_cols = grads.shape
    n_samp, n_feat = lax.axis_size("samp"), lax.axis_size("feat")
    fits = (
        n_feat == 2
        and n_samp >= 4
        and n_samp & (n_samp - 1) == 0
        and feat_cols == n_samp * LANES
        and rows_dev % (2 * LANES) == 0
        and targets.shape[1] % CHUNK == 0
        and targets.shape[1] <= LANES
    )
    return (fused if fits else per_device)(grads, weights, targets)


def solution(mesh):
    return jax.shard_map(
        dispatch,
        mesh=mesh,
        in_specs=(P("samp", "feat"), P("samp"), P("feat", None)),
        out_specs=(P(("samp", "feat"), None), P("feat", None), P("feat", None)),
        check_vma=False,
    )
```

time: 43.8 us -> 41.7 us (0.952)
  Pallas kernels: 42.3 us -> 41 us
  local copies, waits for them, and re-layouts: 0.67 us -> 0 us
    pallas_call x1, Pallas kernels: 41.3 us -> 39.9 us  [fused(): pl.pallas_call(functools.partial(kernel, rows_dev * n_samp, feat_cols * n...]
    unnamed x2 -> x0, local copies, waits for them, and re-layouts: 0.67 us -> none
where the time goes in v2:
time: 41.7 us; the launch traced here: 41.6 us
  Pallas kernels  41 us (98%)
  between operations  0.64 us (2%)
    pallas_call x1, Pallas kernels, fused(): pl.pallas_call(functools.partial(kernel, rows_dev * n_samp, feat_cols * n...  39.9 us
    pallas_call x1, Pallas kernels, write_out(): pl.pallas_call(store_kernel, out_shape=tuple((jax.ShapeDtypeStruct(a.shap...  1.02 us

profile of v2, /device:TPU:0, one launch (start us, length us, event | category | flops | bytes accessed | tf_op | source)
XLA Modules:
  0.0 41.6 jit_solution(14710730672073355507)
XLA Ops:
  0.6 39.9 %cg.1 = (f32[64,256]{1,0:T(8,128)S(1)}, f32[64,2048]{1,0:T(8,128)S(1)}, f32[64,2048]{1,0:T(8,128)S(1)}) custom-call(bf16[512,2048]{1,0:T(8,128)(2,1)} %grads_hbm.1, f32[1,512]{1,0:T(1,128)} %bitcast.6, f32[64,2048]{1,0:T(8,128)} %bitcast.5), custom_call_target="tpu_custom_call" | custom-call | tf_op jit(solution)/shard_map/cg/pallas_call | solution.py:329
  40.6 1.0 %store.1 = (f32[64,256]{1,0:T(8,128)}, f32[64,2048]{1,0:T(8,128)}, f32[64,2048]{1,0:T(8,128)}) custom-call(f32[64,256]{1,0:T(8,128)S(1)} %get-tuple-element.9.refs_0_, f32[64,2048]{1,0:T(8,128)S(1)} %get-tuple-element.10.refs_1_, f32[64,2048]{1,0:T(8,128)S(1)} %get-tuple-element.11.refs_2_), custom_call_target="tpu_custom_call" | custom-call | tf_op jit(solution)/shard_map/store/pallas_call | solution.py:308

commit v3 on v2

--- a/solution.py
+++ b/solution.py
@@ -9,7 +9,10 @@
 from jax.sharding import PartitionSpec as P
 
 ITERS = 2
-CHUNK = 16
+CHUNK = 32
+GATHER_CUTS = (5,)
+PART_HOPS = 4
+TILE_HOPS = 4
 LANES = 128
 VMEM_BYTES = 105 * 2**19
 STORE_BYTES = 2**22
@@ -25,11 +28,12 @@
     grads_ref, weights_ref, targets_ref,
     rows_out, rows_in, first_rows, second_rows,
     norms_out, norms_in, sums_out, sums_in,
-    part_out, part_in, gathered, curve_out, curve_in,
-    load_sem, x_send, x_recv, part_send, part_recv, gather_send, gather_recv, curve_send, curve_recv,
+    swap_out, swap_in, near_f32, near_out, part_out, part_in, gathered, curve_out, curve_in,
+    load_sem, x_send, x_recv, swap_send, swap_recv, part_send, part_recv,
+    gather_send, gather_recv, pass_send, pass_recv, curve_send, curve_recv,
 ):
     samp, feat = lax.axis_index("samp"), lax.axis_index("feat")
-    n_samp = part_in.shape[1]
+    n_samp = curve_in.shape[1]
     chips = n_samp // 2
     core, chip = lax.rem(samp, 2), lax.div(samp, 2)
     dirs = targets_ref.shape[0]
@@ -50,8 +54,11 @@
 
     bits = (chips - 1).bit_length()
     peer_chip = [flipped(chip, j, bits) for j in range(chips)]
-    near_first = sorted(range(chips), key=lambda j: j // 2 + j % 2)
+    near_first = hop_order(chips)
     far_first = near_first[::-1]
+    direct, near = split_hops(chips, PART_HOPS)
+    wide, narrow = split_hops(chips, TILE_HOPS)
+    partner = (chip * 2 + 1 - core, feat)
 
     def peer(j, c):
         to = core if c == 0 else 1 - core
@@ -91,17 +98,28 @@
         elif s == 0:
             src, dst = norms_out.at[rows_of(g)], norms_in.at[rows_of(g)]
         else:
-            src, dst = sums_out.at[rows_of(g)], sums_in.at[rows_of(g)]
+            src, dst = sums_out.at[g, pl.ds(0, 2)], sums_in.at[g, pl.ds(0, 2)]
         return remote(src, dst, x_send.at[s, g, kind], x_recv.at[s, g, kind], mirror)
+
+    def size_of(g):
+        return groups[g].stop - groups[g].start
+
+    def swap_copy(s, g):
+        return remote(
+            swap_out.at[s, 1 - core, :, rows_of(g)], swap_in.at[s, :, rows_of(g)],
+            swap_send.at[s, g], swap_recv.at[s, g], partner)
 
     def part_copy(s, g, j, c):
         to, device = peer(j, c)
-        return remote(
-            part_out.at[s, j, to, rows_of(g)], part_in.at[s, 2 * j + c, rows_of(g)],
-            part_send.at[s, g], part_recv.at[s, g], device)
+        if j in near:
+            place = near.index(j) - 1
+            src, slot = near_out.at[s, place, rows_of(g)], 2 * len(direct) + place
+        else:
+            src, slot = part_out.at[s, direct.index(j), to, rows_of(g)], 2 * direct.index(j) + c
+        return remote(src, part_in.at[s, slot, rows_of(g)], part_send.at[s, g], part_recv.at[s, g], device)
 
     def part_all(s, g):
-        ref = part_in.at[s, pl.ds(1, n_samp - 1), rows_of(g)]
+        ref = part_in.at[s, :, rows_of(g)]
         return remote(ref, ref, part_send.at[s, g], part_recv.at[s, g], mirror)
 
     def tile_copy(s, g, j, c):
@@ -109,12 +127,35 @@
         ref = gathered.at[s, chip, core, rows_of(g)]
         return remote(ref, ref, gather_send.at[s, g], gather_recv.at[s, g, j], device)
 
-    def tile_wait(s, g, j):
+    def tile_sends(s, g):
+        sends = [(j, 0) for j in far_first if j in narrow and j] + [(0, 1)]
+        return [tile_copy(s, g, j, c) for j in wide for c in (0, 1)] + [tile_copy(s, g, j, c) for j, c in sends]
+
+    def pass_copy(s, g, j):
+        ref = gathered.at[s, peer_chip[j], core, rows_of(g)]
+        return remote(ref, ref, pass_send.at[s, g], pass_recv.at[s, g, j], partner)
+
+    def tile_arrival(s, g, j):
         if j == 0:
             ref = gathered.at[s, chip, 1 - core, rows_of(g)]
+        elif j in narrow:
+            ref = gathered.at[s, peer_chip[j], core, rows_of(g)]
         else:
             ref = gathered.at[s, peer_chip[j], pl.ds(0, 2), rows_of(g)]
         remote(ref, ref, gather_send.at[s, g], gather_recv.at[s, g, j], mirror).wait_recv()
+
+    def tile_wait(s, g, j):
+        if j == 0 or j in wide:
+            tile_arrival(s, g, j)
+        else:
+            ref = gathered.at[s, peer_chip[j], 1 - core, rows_of(g)]
+            remote(ref, ref, pass_send.at[s, g], pass_recv.at[s, g, j], partner).wait_recv()
+
+    def forward(s, g):
+        for j in near_first:
+            if j in narrow and j:
+                tile_arrival(s, g, j)
+                pass_copy(s, g, j).start()
 
     def curve_copy(g, j, c):
         to, device = peer(j, c)
@@ -138,6 +179,12 @@
     def diagonal(size):
         shape = (size, LANES)
         return lax.broadcasted_iota(jnp.int32, shape, 0) == lax.broadcasted_iota(jnp.int32, shape, 1)
+
+    def to_line(values, size):
+        return jnp.sum(jnp.where(diagonal(size), values, 0.0), axis=0, keepdims=True)
+
+    def to_column(line, size):
+        return column(jnp.where(diagonal(size), line, 0.0))
 
     loads[0].wait()
     targets = targets_ref[...]
@@ -168,8 +215,8 @@
             x_copy(0, g, 1).wait_recv()
             x_copy(1, g, 1).wait_recv()
             norm0 = column(norms_out[rows, :] + norms_in[rows, :])
-            both = sums_out[rows, :] + sums_in[rows, :]
-            along, square = column(both[:, :LANES]), column(both[:, LANES:])
+            both = sums_out[g, 0:2, :] + sums_in[g, 0:2, :]
+            along, square = [to_column(both[i : i + 1], size_of(g)) for i in range(2)]
             alpha0 = norm0 / along
             cross = norm0 - alpha0 * along
             norm1 = cross - alpha0 * (along - alpha0 * square)
@@ -183,30 +230,42 @@
         weighted = (whole * scaled).astype(b16)
         for j in far_first:
             image = jnp.dot(weighted, grads_ref[:, pair_lanes(j)], preferred_element_type=f32)
-            if j == 0:
-                now["own"] = jnp.where(core == 0, image[:, :LANES], image[:, LANES:])
+            tiles = [image[:, c * LANES : (c + 1) * LANES] for c in range(2)]
+            if j in near:
+                near_f32[near.index(j), rows, :] = jnp.where(core == 0, tiles[0], tiles[1])
             for c in range(2):
-                part_out[s, j, c, rows, :] = image[:, c * LANES : (c + 1) * LANES].astype(b16)
+                if j in near:
+                    swap_out[s, c, near.index(j), rows, :] = tiles[c].astype(b16)
+                else:
+                    part_out[s, direct.index(j), c, rows, :] = tiles[c].astype(b16)
+        swap_copy(s, g).start()
+        for j in direct:
             for c in range(2):
-                if (j, c) != (0, 0):
-                    part_copy(s, g, j, c).start()
+                part_copy(s, g, j, c).start()
         if s == 1:
-            size = rows.stop - rows.start
-            curve = column(lane_sum(weighted.astype(f32) * whole))
-            line = jnp.sum(jnp.where(diagonal(size), curve, 0.0), axis=0, keepdims=True)
+            line = to_line(column(lane_sum(weighted.astype(f32) * whole)), size_of(g))
             curve_out[g, 0:1, :] = line
             curve_in[g, 0:1, :] = line
             for j, c in others:
                 curve_copy(g, j, c).start()
+
+    def swap(s, g):
+        now, rows = state[g], groups[g]
+        swap_copy(s, g).wait_recv()
+        for place, j in reversed(list(enumerate(near))):
+            both = near_f32[place, rows, :] + swap_in[s, place, rows, :].astype(f32)
+            if j:
+                near_out[s, place - 1, rows, :] = both.astype(b16)
+                part_copy(s, g, j, 0).start()
+            else:
+                now["own"] = both
 
     def reduce(s, g):
         now, rows = state[g], groups[g]
         target = targets_ref[rows, own_lanes]
         if s == 1:
             curve_all(g).wait_recv()
-            size = rows.stop - rows.start
-            line = jnp.sum(curve_in[g], axis=0, keepdims=True)
-            curve = column(jnp.where(diagonal(size), line, 0.0))
+            curve = to_column(jnp.sum(curve_in[g], axis=0, keepdims=True), size_of(g))
             now["alpha1"] = now["norm1"] / (curve + damping_term * now["length"])
             resid = target - now["alpha0"] * now["image0"]
             direction = resid + now["ratio"] * target
@@ -214,7 +273,7 @@
             direction = target
         part_all(s, g).wait_recv()
         image = now["own"] + damping_term * direction
-        for k in range(1, n_samp):
+        for k in range(part_in.shape[1]):
             image = image + part_in[s, k, rows, :].astype(f32)
         if s == 0:
             now["image0"] = image
@@ -222,22 +281,26 @@
         else:
             tile = resid - now["alpha1"] * image
         gathered[s, chip, core, rows, :] = tile.astype(b16)
-        for j, c in others:
-            tile_copy(s, g, j, c).start()
+        for copy in tile_sends(s, g):
+            copy.start()
 
     def gather(s, g):
         now, rows = state[g], groups[g]
         if s == 0:
             mine = along = square = 0.0
-            for j in near_first:
-                tile_wait(0, g, j)
+            for place, j in enumerate(near_first):
+                for first, last in zip((0,) + GATHER_CUTS, GATHER_CUTS + (chips,)):
+                    if place == first:
+                        for other in near_first[first:last]:
+                            tile_wait(0, g, other)
                 block = jnp.concatenate([gathered[0, peer_chip[j], c, rows, :] for c in range(2)], axis=1)
                 mine = mine + lax.dot_general(
                     block, grads_ref[:, pair_lanes(j)], nt, preferred_element_type=f32)
                 block = block.astype(f32)
                 along = along + lane_sum(block * targets_ref[rows, pair_lanes(j)])
                 square = square + lane_sum(block * block)
-            sums_out[rows, :] = jnp.concatenate([along, square], axis=1)
+            for i, block in enumerate([along, square]):
+                sums_out[g, i : i + 1, :] = to_line(column(block), size_of(g))
             x_copy(1, g, 1).start()
             rows_out[1, rows, :] = mine.astype(b16)
             x_copy(1, g, 0).start()
@@ -263,34 +326,46 @@
                 solution_ref[rows, lanes] = (
                     start_part * targets_ref[rows, lanes] - image_part * gathered[0, i, c, rows, :].astype(f32))
 
+    stages = dict(exchange=exchange, swap=swap, reduce=reduce, forward=forward, gather=gather, finish=finish)
     for step in order(count):
         stage, *where = step
-        {"exchange": exchange, "reduce": reduce, "gather": gather, "finish": finish}[stage](*where)
+        stages[stage](*where)
     for g in range(count):
         for s in range(ITERS):
             for kind in range(2):
                 x_copy(s, g, kind).wait_send()
+            swap_copy(s, g).wait_send()
             part_all(s, g).wait_send()
-            part_ref = part_in.at[s, pl.ds(1, n_samp - 1), rows_of(g)]
-            remote(part_ref, part_ref, gather_send.at[s, g], gather_send.at[s, g], mirror).wait_send()
+            for copy in tile_sends(s, g):
+                copy.wait_send()
+            for j in narrow:
+                if j:
+                    pass_copy(s, g, j).wait_send()
         curve_all(g).wait_send()
+
+
+def hop_order(chips):
+    return sorted(range(chips), key=hops)
+
+
+def hops(j):
+    return j // 2 + j % 2
+
+
+def split_hops(chips, limit):
+    ordered = hop_order(chips)
+    return [j for j in ordered if hops(j) >= limit], [j for j in ordered if hops(j) < limit]
 
 
 def order(count):
     steps = []
-    all_of = range(count)
-    steps += [("exchange", 0, g) for g in all_of]
-    steps += [("reduce", 0, g) for g in all_of]
-    lag = max(1, count - 1)
-    gathers, exchanges = list(all_of), list(all_of)
-    steps += [("gather", 0, g) for g in gathers[:lag]]
-    for g in exchanges:
-        steps.append(("exchange", 1, g))
-        if lag + g < count:
-            steps.append(("gather", 0, lag + g))
-    steps += [("reduce", 1, g) for g in all_of]
-    steps += [("finish", g) for g in all_of]
-    steps += [("gather", 1, g) for g in all_of]
+    for s in range(ITERS):
+        for stage in ("exchange", "swap", "reduce"):
+            steps += [(stage, s, g) for g in range(count)]
+        if s == ITERS - 1:
+            steps += [("finish", g) for g in range(count)]
+        for stage in ("forward", "gather"):
+            steps += [(stage, s, g) for g in range(count)]
     return steps
 
 
@@ -323,6 +398,7 @@
     dirs = targets.shape[1]
     chips = n_samp // 2
     count = -(-dirs // CHUNK)
+    n_direct, n_near = [len(part) for part in split_hops(chips, PART_HOPS)]
     f32, b16 = jnp.float32, jnp.bfloat16
     vmem = pl.BlockSpec(memory_space=pltpu.VMEM)
     dma = pltpu.SemaphoreType.DMA
@@ -345,16 +421,22 @@
             pltpu.VMEM((dirs, rows_dev), f32),
             pltpu.VMEM((dirs, LANES), f32),
             pltpu.VMEM((dirs, LANES), f32),
-            pltpu.VMEM((dirs, 2 * LANES), f32),
-            pltpu.VMEM((dirs, 2 * LANES), f32),
-            pltpu.VMEM((ITERS, chips, 2, dirs, LANES), b16),
-            pltpu.VMEM((ITERS, n_samp, dirs, LANES), b16),
+            pltpu.VMEM((count, 8, LANES), f32),
+            pltpu.VMEM((count, 8, LANES), f32),
+            pltpu.VMEM((ITERS, 2, n_near, dirs, LANES), b16),
+            pltpu.VMEM((ITERS, n_near, dirs, LANES), b16),
+            pltpu.VMEM((n_near, dirs, LANES), f32),
+            pltpu.VMEM((ITERS, max(1, n_near - 1), dirs, LANES), b16),
+            pltpu.VMEM((ITERS, max(1, n_direct), 2, dirs, LANES), b16),
+            pltpu.VMEM((ITERS, 2 * n_direct + n_near - 1, dirs, LANES), b16),
             pltpu.VMEM((ITERS, chips, 2, dirs, LANES), b16),
             pltpu.VMEM((count, 8, LANES), f32),
             pltpu.VMEM((count, n_samp, LANES), f32),
             dma((4,)),
             dma((ITERS, count, 2)), dma((ITERS, count, 2)),
             dma((ITERS, count)), dma((ITERS, count)),
+            dma((ITERS, count)), dma((ITERS, count)),
+            dma((ITERS, count)), dma((ITERS, count, chips)),
             dma((ITERS, count)), dma((ITERS, count, chips)),
             dma((count,)), dma((count,)),
         ],

time: 41.7 us -> 39.1 us (0.938)
  Pallas kernels: 41 us -> 38.3 us
    pallas_call x1, Pallas kernels: 39.9 us -> 37.3 us  [fused(): pl.pallas_call(functools.partial(kernel, rows_dev * n_samp, feat_cols * n...]
where the time goes in v3:
time: 39.1 us; the launch traced here: 38.9 us
  Pallas kernels  38.3 us (98%)
  between operations  0.64 us (2%)
    pallas_call x1, Pallas kernels, fused(): pl.pallas_call(functools.partial(kernel, rows_dev * n_samp, feat_cols * n...  37.3 us
    pallas_call x1, Pallas kernels, write_out(): pl.pallas_call(store_kernel, out_shape=tuple((jax.ShapeDtypeStruct(a.shap...  1.02 us

profile of v3, /device:TPU:0, one launch (start us, length us, event | category | flops | bytes accessed | tf_op | source)
XLA Modules:
  0.0 38.9 jit_solution(5785814737968943646)
XLA Ops:
  0.6 37.3 %cg.1 = (f32[64,256]{1,0:T(8,128)S(1)}, f32[64,2048]{1,0:T(8,128)S(1)}, f32[64,2048]{1,0:T(8,128)S(1)}) custom-call(bf16[512,2048]{1,0:T(8,128)(2,1)} %grads_hbm.1, f32[1,512]{1,0:T(1,128)} %bitcast.6, f32[64,2048]{1,0:T(8,128)} %bitcast.5), custom_call_target="tpu_custom_call" | custom-call | tf_op jit(solution)/shard_map/cg/pallas_call | solution.py:405
  37.9 1.0 %store.1 = (f32[64,256]{1,0:T(8,128)}, f32[64,2048]{1,0:T(8,128)}, f32[64,2048]{1,0:T(8,128)}) custom-call(f32[64,256]{1,0:T(8,128)S(1)} %get-tuple-element.9.refs_0_, f32[64,2048]{1,0:T(8,128)S(1)} %get-tuple-element.10.refs_1_, f32[64,2048]{1,0:T(8,128)S(1)} %get-tuple-element.11.refs_2_), custom_call_target="tpu_custom_call" | custom-call | tf_op jit(solution)/shard_map/store/pallas_call | solution.py:383

commit v4 on v3

--- a/solution.py
+++ b/solution.py
@@ -10,9 +10,9 @@
 
 ITERS = 2
 CHUNK = 32
-GATHER_CUTS = (5,)
-PART_HOPS = 4
-TILE_HOPS = 4
+PART_HOPS = 5
+TILE_HOPS = 5
+EARLY_HOPS = 2
 LANES = 128
 VMEM_BYTES = 105 * 2**19
 STORE_BYTES = 2**22
@@ -151,8 +151,11 @@
             ref = gathered.at[s, peer_chip[j], 1 - core, rows_of(g)]
             remote(ref, ref, pass_send.at[s, g], pass_recv.at[s, g, j], partner).wait_recv()
 
-    def forward(s, g):
-        for j in near_first:
+    early = [j for j in near_first if hops(j) < EARLY_HOPS]
+    parts = [early, [j for j in near_first if j not in early]]
+
+    def forward(s, g, part):
+        for j in parts[part]:
             if j in narrow and j:
                 tile_arrival(s, g, j)
                 pass_copy(s, g, j).start()
@@ -284,33 +287,32 @@
         for copy in tile_sends(s, g):
             copy.start()
 
-    def gather(s, g):
+    def gather(s, g, part):
         now, rows = state[g], groups[g]
-        if s == 0:
-            mine = along = square = 0.0
-            for place, j in enumerate(near_first):
-                for first, last in zip((0,) + GATHER_CUTS, GATHER_CUTS + (chips,)):
-                    if place == first:
-                        for other in near_first[first:last]:
-                            tile_wait(0, g, other)
-                block = jnp.concatenate([gathered[0, peer_chip[j], c, rows, :] for c in range(2)], axis=1)
-                mine = mine + lax.dot_general(
-                    block, grads_ref[:, pair_lanes(j)], nt, preferred_element_type=f32)
-                block = block.astype(f32)
-                along = along + lane_sum(block * targets_ref[rows, pair_lanes(j)])
-                square = square + lane_sum(block * block)
-            for i, block in enumerate([along, square]):
-                sums_out[g, i : i + 1, :] = to_line(column(block), size_of(g))
-            x_copy(1, g, 1).start()
-            rows_out[1, rows, :] = mine.astype(b16)
-            x_copy(1, g, 0).start()
-            second_rows[rows, :] = mine
-        else:
-            for j in near_first:
-                tile_wait(1, g, j)
+        for j in parts[part]:
+            tile_wait(s, g, j)
+        if s == 1:
+            for j in parts[part]:
                 for c in range(2):
                     lanes = pl.ds(pl.multiple_of(peer_chip[j] * pair + c * LANES, LANES), LANES)
                     resid_ref[rows, lanes] = gathered[1, peer_chip[j], c, rows, :].astype(f32)
+            return
+        mine, along, square = now.get("sums", (0.0, 0.0, 0.0))
+        for j in parts[part]:
+            block = jnp.concatenate([gathered[0, peer_chip[j], c, rows, :] for c in range(2)], axis=1)
+            mine = mine + lax.dot_general(block, grads_ref[:, pair_lanes(j)], nt, preferred_element_type=f32)
+            block = block.astype(f32)
+            along = along + lane_sum(block * targets_ref[rows, pair_lanes(j)])
+            square = square + lane_sum(block * block)
+        if part == 0:
+            now["sums"] = (mine, along, square)
+            return
+        for i, block in enumerate([along, square]):
+            sums_out[g, i : i + 1, :] = to_line(column(block), size_of(g))
+        x_copy(1, g, 1).start()
+        rows_out[1, rows, :] = mine.astype(b16)
+        x_copy(1, g, 0).start()
+        second_rows[rows, :] = mine
 
     def finish(g):
         now, rows = state[g], groups[g]
@@ -358,14 +360,21 @@
 
 
 def order(count):
-    steps = []
+    every = range(count)
+    steps = [(stage, 0, g) for stage in ("exchange", "swap") for g in every]
     for s in range(ITERS):
-        for stage in ("exchange", "swap", "reduce"):
-            steps += [(stage, s, g) for g in range(count)]
+        if s == 1:
+            steps += [(stage, s, g) for g in every for stage in ("exchange", "swap")]
+        steps += [("reduce", s, g) for g in every]
         if s == ITERS - 1:
-            steps += [("finish", g) for g in range(count)]
-        for stage in ("forward", "gather"):
-            steps += [(stage, s, g) for g in range(count)]
+            steps += [("finish", g) for g in every]
+        steps += [("forward", s, 0, 0), ("forward", s, 0, 1)]
+        for g in every:
+            if g + 1 < count:
+                steps.append(("forward", s, g + 1, 0))
+            steps += [("gather", s, g, 0), ("gather", s, g, 1)]
+            if g + 1 < count:
+                steps.append(("forward", s, g + 1, 1))
     return steps
 
 

time: 39.1 us -> 37.4 us (0.957)
  Pallas kernels: 38.3 us -> 36.6 us
    pallas_call x1, Pallas kernels: 37.3 us -> 35.6 us  [fused(): pl.pallas_call(functools.partial(kernel, rows_dev * n_samp, feat_cols * n...]
where the time goes in v4:
time: 37.4 us; the launch traced here: 37.2 us
  Pallas kernels  36.6 us (98%)
  between operations  0.64 us (2%)
    pallas_call x1, Pallas kernels, fused(): pl.pallas_call(functools.partial(kernel, rows_dev * n_samp, feat_cols * n...  35.6 us
    pallas_call x1, Pallas kernels, write_out(): pl.pallas_call(store_kernel, out_shape=tuple((jax.ShapeDtypeStruct(a.shap...  1.02 us

profile of v4, /device:TPU:0, one launch (start us, length us, event | category | flops | bytes accessed | tf_op | source)
XLA Modules:
  0.0 37.2 jit_solution(8626204143666133798)
XLA Ops:
  0.6 35.6 %cg.1 = (f32[64,256]{1,0:T(8,128)S(1)}, f32[64,2048]{1,0:T(8,128)S(1)}, f32[64,2048]{1,0:T(8,128)S(1)}) custom-call(bf16[512,2048]{1,0:T(8,128)(2,1)} %grads_hbm.1, f32[1,512]{1,0:T(1,128)} %bitcast.6, f32[64,2048]{1,0:T(8,128)} %bitcast.5), custom_call_target="tpu_custom_call" | custom-call | tf_op jit(solution)/shard_map/cg/pallas_call | solution.py:414
  36.2 1.0 %store.1 = (f32[64,256]{1,0:T(8,128)}, f32[64,2048]{1,0:T(8,128)}, f32[64,2048]{1,0:T(8,128)}) custom-call(f32[64,256]{1,0:T(8,128)S(1)} %get-tuple-element.9.refs_0_, f32[64,2048]{1,0:T(8,128)S(1)} %get-tuple-element.10.refs_1_, f32[64,2048]{1,0:T(8,128)S(1)} %get-tuple-element.11.refs_2_), custom_call_target="tpu_custom_call" | custom-call | tf_op jit(solution)/shard_map/store/pallas_call | solution.py:392
